TPU v7x, 512 devices: a whole 4x4x16 slice. The times are simulated.
512 devices in a mesh: grp: 16 (over z), cand: 32 (over y, x, core).
Axes of the slice: x: 4, y: 4, z: 16, core: 2. Of those that a mesh axis runs over, the one named last changes fastest.
Arguments:
- embeddings: bfloat16 [384, 1024, 1024], P('grp', 'cand'), may hold values from -6 to 6
- hidden_weight: bfloat16 [2048, 1024], P('cand'), may hold values from -0.1875 to 0.1875
- score_weight: bfloat16 [2048], replicated, may hold values from -0.5 to 0.5
- relevance: int32 [384, 1024], P('grp', 'cand'), may hold values from 0 to 4
- rank_pos: int32 [384, 1024], P('grp', 'cand'), may hold values from 0 to 1023, as said below
- ideal_dcg: float32 [384], P('grp'), may hold values from 32 to 128
Outputs:
- grad_hidden: float32 [2048, 1024], P('cand')
- lambdas: float32 [384, 1024], P('grp', 'cand')
Inputs may be any that keep to these rules, and one draw needn't show every extreme that they name: `rank_pos`: in each group the rank positions are a permutation of 0 to 1023.
All inputs are finite; a program needn't handle non-finite values.
Results may differ from a plain program's by a relative error of at most 0.006.
Values may be sent and summed in bfloat16 or wider, within the bound.
No kernel may reach another device: no remote copies, remote signals or barrier semaphores. Data moves between devices by JAX's collectives and lax.ppermute only.
A program may use at most 64 MiB of HBM per device.

v0:
```python
import jax
import jax.numpy as jnp
from jax import lax
from jax.sharding import PartitionSpec as P

EPS = 1e-06


def turned_gather(arrays, axis, dims):
    turned = [jnp.moveaxis(a, dim, 0) for a, dim in zip(arrays, dims)]
    widths = [t[0].size for t in turned]
    both = jnp.concatenate([t.reshape(-1, w) for t, w in zip(turned, widths)], axis=1)
    result = lax.all_gather(both, axis, axis=0, tiled=True)
    parts = jnp.split(result, [sum(widths[:k]) for k in range(1, len(widths))], axis=1)
    return tuple(
        (
            jnp.moveaxis(b.reshape(-1, *t.shape[1:]), 0, dim)
            for b, t, dim in zip(parts, turned, dims)
        )
    )


def copy_for_each(value, axis):
    copies = jnp.broadcast_to(value, (lax.axis_size(axis), *value.shape))
    return lax.all_to_all(copies, axis, split_axis=0, concat_axis=0, tiled=True)


def joined_along(parts, dim):
    parts = jnp.moveaxis(parts, 0, dim)
    shape = parts.shape
    return parts.reshape(*shape[:dim], shape[dim] * shape[dim + 1], *shape[dim + 2 :])


def gathered_copies(value, axis, dim):
    parts = copy_for_each(value, axis)
    return joined_along(parts, dim)


def over_copies(value, axis):
    return copy_for_each(value, axis).sum(axis=0)


def pair_lambdas(own_score, own_gain, own_disc, far_score, far_gain, far_disc, ideal):
    gain_diff = far_gain[..., None, :] - own_gain[..., :, None]
    toward = jnp.sign(gain_diff)
    weight = (
        jnp.abs(gain_diff)
        * jnp.abs(far_disc[..., None, :] - own_disc[..., :, None])
        / ideal[..., None, None]
    )
    margin = own_score[..., :, None] - far_score[..., None, :]
    return jnp.sum(weight * toward * jax.nn.sigmoid(toward * margin), axis=-1)


def gain_of(labels):
    return jnp.exp2(labels.astype(jnp.float32)) - 1.0


def discount_of(positions):
    return 1.0 / jnp.log2(2.0 + positions.astype(jnp.float32))


def per_device(embeddings, hidden_weight, score_weight, relevance, rank_pos, ideal_dcg):
    grp_count, local, width = embeddings.shape
    cand_rows = embeddings.reshape(grp_count * local, width)
    all_labels, all_ranks = turned_gather((relevance, rank_pos), "cand", (1, 1))
    all_gain = gain_of(all_labels)
    all_disc = discount_of(all_ranks)
    pre_act = lax.dot_general(
        cand_rows,
        lax.all_gather(hidden_weight, "cand", axis=0, tiled=True),
        (((1,), (1,)), ((), ())),
        preferred_element_type=jnp.float32,
    )
    acts, pull = jax.vjp(jax.nn.gelu, pre_act)
    scores = jnp.dot(
        acts.astype(jnp.bfloat16), score_weight, preferred_element_type=jnp.float32
    ).reshape(grp_count, local)
    gain_vals = gain_of(relevance)
    discount = discount_of(rank_pos)
    lambdas = pair_lambdas(
        scores,
        gain_vals,
        discount,
        gathered_copies(scores, "cand", 1),
        all_gain,
        all_disc,
        ideal_dcg,
    )
    upstream = (
        lambdas.reshape(grp_count * local)[:, None] * score_weight.astype(jnp.float32)[None, :]
    )
    grad_pre = pull(upstream)[0].astype(jnp.bfloat16)
    owned = lax.psum_scatter(
        lax.dot_general(
            grad_pre, cand_rows, (((0,), (0,)), ((), ())), preferred_element_type=jnp.float32
        ).astype(jnp.bfloat16),
        "cand",
        scatter_dimension=0,
        tiled=True,
    ).astype(jnp.float32)
    summed = lax.psum(owned, "grp")
    squares = over_copies(jnp.sum(summed * summed), "cand")
    entries = summed.shape[0] * summed.shape[1] * lax.axis_size("cand")
    scale = lax.rsqrt(squares / entries + EPS)
    return (summed * scale, lambdas)


def solution(mesh):
    return jax.shard_map(
        per_device,
        mesh=mesh,
        in_specs=(
            P("grp", "cand", None),
            P("cand", None),
            P(),
            P("grp", "cand"),
            P("grp", "cand"),
            P("grp"),
        ),
        out_specs=(P("cand", None), P("grp", "cand")),
        check_vma=False,
    )
```

profile of v0, /device:TPU:1, one launch (start us, length us, event | category | flops | bytes accessed | tf_op | source)
XLA Modules:
  0.0 302.9 jit_solution(5547443069772350048)
XLA Ops:
  7.2 0.7 all-gather.2.cloned.1.call-update
  7.9 0.7 reshape.20
  8.6 0.8 copy.28
  9.4 0.8 copy.29
  10.2 28.5 %all_gather.6 = s32[1024,48]{1,0:T(8,128)S(1)} all-gather(s32[32,48]{1,0:T(8,128)S(1)} %pad_add_fusion), channel_id=1, replica_groups=mesh['grp'=16,'cand'=32] {'cand'}, dimensions={0}, use_global_device_ids=true | all-gather | bytes 202752 | tf_op jit(solution)/shard_map/all_gather | solution.py:13
  38.7 0.2 fusion.33
  39.3 38.9 %all-gather.2.cloned.1.call-done = bf16[2048,1024]{1,0:T(8,128)(2,1)} async-done(((bf16[64,1024]{1,0:T(8,128)(2,1)}), bf16[2048,1024]{1,0:T(8,128)(2,1)}) %all-gather.2.cloned.1.call-update) | async-done | bytes 4194320 | tf_op jit(solution)/shard_map/all_gather | solution.py:71
  78.2 5.3 %fusion.34 = f32[768,2048]{1,0:T(8,128)S(1)} fusion(bf16[768,1024]{1,0:T(8,128)(2,1)S(1)} %bitcast.12, bf16[2048,1024]{1,0:T(8,128)(2,1)} %all-gather.2.cloned.1.call-done), kind=kOutput, calls=%fused_computation.48 | convolution fusion | flops 3221225472 | bytes 12058624 | tf_op jit(solution)/shard_map/dot_general | solution.py:69
  83.5 2.7 copy-done.6
  86.1 2.2 fusion.22
  88.5 0.8 reshape.24
  89.3 5.3 %all-to-all-start = ((f32[32,1,768]{2,1,0:T(1,128)}), f32[32,1,768]{2,1,0:T(1,128)S(1)}, u32[]{:S(2)}, u32[]{:S(2)}) async-start(f32[32,1,768]{2,1,0:T(1,128)} %reshape.24), calls=%async_computation | async-start | bytes 196608 | tf_op jit(solution)/shard_map/all_to_all | solution.py:25
  94.7 7.3 %all-to-all-done = f32[32,1,768]{2,1,0:T(1,128)S(1)} async-done(((f32[32,1,768]{2,1,0:T(1,128)}), f32[32,1,768]{2,1,0:T(1,128)S(1)}, u32[]{:S(2)}, u32[]{:S(2)}) %all-to-all-start) | async-done | bytes 98336 | tf_op jit(solution)/shard_map/all_to_all | solution.py:25
  102.0 0.5 broadcast.84
  102.5 0.9 reduce.3
  103.8 3.0 fusion.13
  106.9 10.4 %convolution_convert_fusion = bf16[2048,1024]{1,0:T(8,128)(2,1)} fusion(bf16[768,1024]{1,0:T(8,128)(2,1)S(1)} %bitcast.13, f32[768,2048]{1,0:T(8,128)} %copy-done.6, f32[2048]{0:T(1024)S(1)} %convert_element_type.34, f32[768]{0:T(1024)S(1)} %mul.88), kind=kOutput, calls=%fused_computation.19 | convolution fusion | flops 3256352768 | bytes 12069888 | tf_op jit(solution)/shard_map/dot_general | solution.py:95
  117.3 101.5 %reduce-scatter.2.cloned.1.call-done = bf16[64,1024]{1,0:T(8,128)(2,1)} async-done(((bf16[2048,1024]{1,0:T(8,128)(2,1)}), bf16[64,1024]{1,0:T(8,128)(2,1)}) %reduce-scatter.2.cloned.1.call-update) | async-done | bytes 131088 | tf_op jit(solution)/shard_map/reduce_scatter | solution.py:94
  218.8 46.8 %all-reduce.1 = f32[64,1024]{1,0:T(8,128)S(1)} all-reduce(bf16[64,1024]{1,0:T(8,128)(2,1)} %reduce-scatter.2.cloned.1.call-done), channel_id=1, replica_groups=mesh['grp'=16,'cand'=32] {'grp'}, use_global_device_ids=true, to_apply=%region_2.0 | all-reduce | flops 65536 | bytes 393216 | tf_op jit(solution)/shard_map/psum | solution.py:102
  265.6 0.7 multiply_reduce_fusion
  266.2 0.7 broadcast_in_dim.5
  266.9 27.1 %all_to_all.11 = f32[32,1,1]{2,1,0:T(1,128)S(1)} all-to-all(f32[32,1,1]{2,1,0:T(1,128)S(1)} %broadcast_in_dim.5), channel_id=1, replica_groups=mesh['grp'=16,'cand'=32] {'cand'}, dimensions={0} | all-to-all | bytes 256 | tf_op jit(solution)/shard_map/all_to_all | solution.py:25
  294.0 0.6 reduce_sum.29
  295.4 0.7 broadcast_multiply_fusion
  (28 shorter events, 1.2 us)
Async XLA Ops:
  7.2 71.0 %copy-start = (bf16[24,32,1024]{2,1,0:T(8,128)(2,1)S(1)}, bf16[24,32,1024]{2,1,0:T(8,128)(2,1)}, u32[]{:S(2)}) copy-start(bf16[24,32,1024]{2,1,0:T(8,128)(2,1)} %param.6) | copy-start | bytes 4718596
  7.2 71.0 %all-gather.2.cloned.1.call-start = ((), (), s32[]{:S(2)}) async-start(), calls=%async_computation.3 | async-start | bytes 4325376 | tf_op jit(solution)/shard_map/all_gather | solution.py:71
  83.5 2.7 copy-start.6
  86.1 8.6 %copy-start.1 = (s32[24,32]{1,0:T(8,128)S(1)}, s32[24,32]{1,0:T(8,128)}, u32[]{:S(2)}) copy-start(s32[24,32]{1,0:T(8,128)} %param.10) | copy-start | bytes 9220
  86.1 8.6 %copy-start.2 = (s32[24,32]{1,0:T(8,128)S(1)}, s32[24,32]{1,0:T(8,128)}, u32[]{:S(2)}) copy-start(s32[24,32]{1,0:T(8,128)} %param.9) | copy-start | bytes 9220
  86.1 8.6 %copy-start.3 = (bf16[2048]{0:T(1024)(128)(2,1)S(1)}, bf16[2048]{0:T(1024)(128)(2,1)}, u32[]{:S(2)}) copy-start(bf16[2048]{0:T(1024)(128)(2,1)} %param.8) | copy-start | bytes 12292
  86.1 17.7 %copy-start.5 = (f32[24]{0:T(128)S(1)}, f32[24]{0:T(128)}, u32[]{:S(2)}) copy-start(f32[24]{0:T(128)} %param.11) | copy-start | bytes 292
  89.3 12.7 %all-to-all-start = ((f32[32,1,768]{2,1,0:T(1,128)}), f32[32,1,768]{2,1,0:T(1,128)S(1)}, u32[]{:S(2)}, u32[]{:S(2)}) async-start(f32[32,1,768]{2,1,0:T(1,128)} %reshape.24), calls=%async_computation | async-start | bytes 196608 | tf_op jit(solution)/shard_map/all_to_all | solution.py:25
  94.6 124.2 %reduce-scatter.2.cloned.1.call-start = ((), (), s32[]{:S(2)}) async-start(), calls=%async_computation.4 | async-start | bytes 4325376 | tf_op jit(solution)/shard_map/reduce_scatter | solution.py:94
  106.8 10.5 %copy-start.4 = (f32[24,32]{1,0:T(8,128)}, f32[24,32]{1,0:T(8,128)S(1)}, u32[]{:S(2)}) copy-start(f32[24,32]{1,0:T(8,128)S(1)} %fusion.13) | copy-start | bytes 9220
Sparse Core Ops, SparseCore 0:
  11.1 67.0 all-gather.1
  117.5 101.2 reduce-scatter.1
where the time goes:
time: 303 us
  waiting for transfers between devices  148 us (49%)
  blocking collectives  102 us (34%)
  matrix products  17.9 us (6%)
  between operations  14.9 us (5%)
  local copies, waits for them, and re-layouts  8.06 us (3%)
  other arithmetic  6.06 us (2%)
  starting transfers between devices  5.38 us (2%)
    reduce_scatter x1, waiting for transfers between devices, per_device(): lax.psum_scatter(lax.dot_general(grad_pre, cand_rows, (((0,), (0,)), ((),...  101 us
    psum x1, blocking collectives, per_device(): summed = lax.psum(owned, 'grp')  46.8 us
    all_gather x1, waiting for transfers between devices, per_device(): lax.all_gather(hidden_weight, 'cand', axis=0, tiled=True)  38.9 us
    all_gather x1, blocking collectives, turned_gather(): result = lax.all_gather(both, axis, axis=0, tiled=True)  28.5 us
    all_to_all x1, blocking collectives, copy_for_each(): return lax.all_to_all(copies, axis, split_axis=0, concat_axis=0, tiled=True)  27.1 us
    dot_general x1, matrix products, per_device(): lax.dot_general(grad_pre, cand_rows, (((0,), (0,)), ((), ())), preferred_...  10.4 us
    all_to_all x1, waiting for transfers between devices, copy_for_each(): return lax.all_to_all(copies, axis, split_axis=0, concat_axis=0, tiled=True)  7.27 us
    unnamed x21, local copies, waits for them, and re-layouts  6.27 us
  transfers between devices with their start and end apart: 3, of which 3 were waited for; matrix products, arithmetic and copies ran while one was open for 1% of the time, Pallas kernels for 0%

commit v1 on v0

--- a/solution.py
+++ b/solution.py
@@ -61,6 +61,16 @@
 
 
 def per_device(embeddings, hidden_weight, score_weight, relevance, rank_pos, ideal_dcg):
+
+    def cover_bands(unit):
+        chip_axis = "grp"
+        world = lax.axis_size(chip_axis)
+        big = lambda side_arr: [(rr, rr ^ side_arr) for rr in range(world)]
+        aux = unit
+        for i0 in range(world.bit_length() - 1):
+            aux = aux + lax.ppermute(aux, chip_axis, big(1 << i0))
+        return aux
+
     grp_count, local, width = embeddings.shape
     cand_rows = embeddings.reshape(grp_count * local, width)
     all_labels, all_ranks = turned_gather((relevance, rank_pos), "cand", (1, 1))
@@ -99,7 +109,7 @@
         scatter_dimension=0,
         tiled=True,
     ).astype(jnp.float32)
-    summed = lax.psum(owned, "grp")
+    summed = cover_bands(owned)
     squares = over_copies(jnp.sum(summed * summed), "cand")
     entries = summed.shape[0] * summed.shape[1] * lax.axis_size("cand")
     scale = lax.rsqrt(squares / entries + EPS)

time: 303 us -> 327 us (1.079)
  blocking collectives: 102 us -> 40.5 us
  waiting for transfers between devices: 148 us -> 201 us
  starting transfers between devices: 5.38 us -> 36.6 us
    ppermute x0 -> x4, waiting for transfers between devices: none -> 52.2 us  [cover_bands(): aux = aux + lax.ppermute(aux, chip_axis, big(1 << i0))]
    psum x1 -> x0, blocking collectives: 46.8 us -> none  [per_device(): summed = lax.psum(owned, 'grp')]
    ppermute x0 -> x4, starting transfers between devices: none -> 31.2 us  [cover_bands(): aux = aux + lax.ppermute(aux, chip_axis, big(1 << i0))]
    all_to_all x1, blocking collectives: 27.1 us -> 12 us  [copy_for_each(): return lax.all_to_all(copies, axis, split_axis=0, concat_axis=0, tiled=True)]
  transfers between devices with their start and end apart: 3 -> 7, of which waited for: 3 -> 7; matrix products, arithmetic and copies ran while one was open for 1% -> 1% of each run, Pallas kernels for 0% -> 0%
where the time goes in v1:
time: 327 us; the launch traced here: 326 us
  waiting for transfers between devices  201 us (61%)
  blocking collectives  40.5 us (12%)
  starting transfers between devices  36.6 us (11%)
  matrix products  17.9 us (5%)
  between operations  14.9 us (5%)
  local copies, waits for them, and re-layouts  8.05 us (2%)
  other arithmetic  7.98 us (2%)
    reduce_scatter x1, waiting for transfers between devices, per_device(): lax.psum_scatter(lax.dot_general(grad_pre, cand_rows, (((0,), (0,)), ((),...  101 us
    ppermute x4, waiting for transfers between devices, cover_bands(): aux = aux + lax.ppermute(aux, chip_axis, big(1 << i0))  52.2 us
    all_gather x1, waiting for transfers between devices, per_device(): lax.all_gather(hidden_weight, 'cand', axis=0, tiled=True)  38.8 us
    ppermute x4, starting transfers between devices, cover_bands(): aux = aux + lax.ppermute(aux, chip_axis, big(1 << i0))  31.2 us
    all_gather x1, blocking collectives, turned_gather(): result = lax.all_gather(both, axis, axis=0, tiled=True)  28.5 us
    all_to_all x1, blocking collectives, copy_for_each(): return lax.all_to_all(copies, axis, split_axis=0, concat_axis=0, tiled=True)  12 us
    dot_general x1, matrix products, per_device(): lax.dot_general(grad_pre, cand_rows, (((0,), (0,)), ((), ())), preferred_...  10.4 us
    all_to_all x1, waiting for transfers between devices, copy_for_each(): return lax.all_to_all(copies, axis, split_axis=0, concat_axis=0, tiled=True)  7.27 us
  transfers between devices with their start and end apart: 7, of which 7 were waited for; matrix products, arithmetic and copies ran while one was open for 1% of the time, Pallas kernels for 0%

profile of v1, /device:TPU:1, one launch (start us, length us, event | category | flops | bytes accessed | tf_op | source)
XLA Modules:
  0.0 326.5 jit_solution(2660351963352656586)
XLA Ops:
  9.4 0.8 copy.29
  10.2 28.5 %all_gather.6 = s32[1024,48]{1,0:T(8,128)S(1)} all-gather(s32[32,48]{1,0:T(8,128)S(1)} %pad_add_fusion), channel_id=1, replica_groups=mesh['grp'=16,'cand'=32] {'cand'}, dimensions={0}, use_global_device_ids=true | all-gather | bytes 202752 | tf_op jit(solution)/shard_map/all_gather | solution.py:13
  39.3 38.8 %all-gather.2.cloned.1.call-done = bf16[2048,1024]{1,0:T(8,128)(2,1)} async-done(((bf16[64,1024]{1,0:T(8,128)(2,1)}), bf16[2048,1024]{1,0:T(8,128)(2,1)}) %all-gather.2.cloned.1.call-update) | async-done | bytes 4194320 | tf_op jit(solution)/shard_map/all_gather | solution.py:81
  78.2 5.3 %fusion.34 = f32[768,2048]{1,0:T(8,128)S(1)} fusion(bf16[768,1024]{1,0:T(8,128)(2,1)S(1)} %bitcast.12, bf16[2048,1024]{1,0:T(8,128)(2,1)} %all-gather.2.cloned.1.call-done), kind=kOutput, calls=%fused_computation.49 | convolution fusion | flops 3221225472 | bytes 12058624 | tf_op jit(solution)/shard_map/dot_general | solution.py:79
  83.5 2.6 copy-done.6
  86.1 2.2 fusion.22
  88.5 0.8 reshape.24
  89.3 5.3 %all-to-all-start = ((f32[32,1,768]{2,1,0:T(1,128)}), f32[32,1,768]{2,1,0:T(1,128)S(1)}, u32[]{:S(2)}, u32[]{:S(2)}) async-start(f32[32,1,768]{2,1,0:T(1,128)} %reshape.24), calls=%async_computation | async-start | bytes 196608 | tf_op jit(solution)/shard_map/all_to_all | solution.py:25
  94.7 7.3 %all-to-all-done = f32[32,1,768]{2,1,0:T(1,128)S(1)} async-done(((f32[32,1,768]{2,1,0:T(1,128)}), f32[32,1,768]{2,1,0:T(1,128)S(1)}, u32[]{:S(2)}, u32[]{:S(2)}) %all-to-all-start) | async-done | bytes 98336 | tf_op jit(solution)/shard_map/all_to_all | solution.py:25
  102.5 0.9 reduce.3
  103.8 3.0 fusion.13
  106.9 10.4 %convolution_convert_fusion = bf16[2048,1024]{1,0:T(8,128)(2,1)} fusion(bf16[768,1024]{1,0:T(8,128)(2,1)S(1)} %bitcast.13, f32[768,2048]{1,0:T(8,128)} %copy-done.6, f32[2048]{0:T(1024)S(1)} %convert_element_type.34, f32[768]{0:T(1024)S(1)} %mul.88), kind=kOutput, calls=%fused_computation.19 | convolution fusion | flops 3256352768 | bytes 12069888 | tf_op jit(solution)/shard_map/dot_general | solution.py:105
  117.3 101.5 %reduce-scatter.2.cloned.1.call-done = bf16[64,1024]{1,0:T(8,128)(2,1)} async-done(((bf16[2048,1024]{1,0:T(8,128)(2,1)}), bf16[64,1024]{1,0:T(8,128)(2,1)}) %reduce-scatter.2.cloned.1.call-update) | async-done | bytes 131088 | tf_op jit(solution)/shard_map/reduce_scatter | solution.py:104
  218.8 0.9 convert_element_type.37
  219.7 3.2 collective-permute-start
  222.9 3.9 %collective-permute-done = f32[64,1024]{1,0:T(8,128)S(1)} collective-permute-done((f32[64,1024]{1,0:T(8,128)S(1)}, f32[64,1024]{1,0:T(8,128)S(1)}, u32[]{:S(2)}, u32[]{:S(2)}) %collective-permute-start) | collective-permute-done | bytes 262176 | tf_op jit(solution)/shard_map/ppermute | solution.py:71
  226.8 0.9 convert_add_fusion
  227.8 4.2 %collective-permute-start.1 = (f32[64,1024]{1,0:T(8,128)S(1)}, f32[64,1024]{1,0:T(8,128)S(1)}, u32[]{:S(2)}, u32[]{:S(2)}) collective-permute-start(f32[64,1024]{1,0:T(8,128)S(1)} %convert_add_fusion), channel_id=1, source_target_pairs={{0,64},{32,96},{64,0},{96,32},{128,192},{160,224},{192,128},{224,1... | collective-permute-start | bytes 786440 | tf_op jit(solution)/shard_map/ppermute | solution.py:71
  231.9 11.4 %collective-permute-done.1 = f32[64,1024]{1,0:T(8,128)S(1)} collective-permute-done((f32[64,1024]{1,0:T(8,128)S(1)}, f32[64,1024]{1,0:T(8,128)S(1)}, u32[]{:S(2)}, u32[]{:S(2)}) %collective-permute-start.1) | collective-permute-done | bytes 262176 | tf_op jit(solution)/shard_map/ppermute | solution.py:71
  243.4 7.4 %collective-permute-start.2 = (f32[64,1024]{1,0:T(8,128)S(1)}, f32[64,1024]{1,0:T(8,128)S(1)}, u32[]{:S(2)}, u32[]{:S(2)}) collective-permute-start(f32[64,1024]{1,0:T(8,128)S(1)} %add.51), channel_id=1, source_target_pairs={{0,128},{32,160},{64,192},{96,224},{128,0},{160,32},{192,64},{224,... | collective-permute-start | bytes 786440 | tf_op jit(solution)/shard_map/ppermute | solution.py:71
  250.7 22.6 %collective-permute-done.2 = f32[64,1024]{1,0:T(8,128)S(1)} collective-permute-done((f32[64,1024]{1,0:T(8,128)S(1)}, f32[64,1024]{1,0:T(8,128)S(1)}, u32[]{:S(2)}, u32[]{:S(2)}) %collective-permute-start.2) | collective-permute-done | bytes 262176 | tf_op jit(solution)/shard_map/ppermute | solution.py:71
  273.4 16.5 %collective-permute-start.3 = (f32[64,1024]{1,0:T(8,128)S(1)}, f32[64,1024]{1,0:T(8,128)S(1)}, u32[]{:S(2)}, u32[]{:S(2)}) collective-permute-start(f32[64,1024]{1,0:T(8,128)S(1)} %add.52), channel_id=1, source_target_pairs={{0,256},{32,288},{64,320},{96,352},{128,384},{160,416},{192,448},{... | collective-permute-start | bytes 786440 | tf_op jit(solution)/shard_map/ppermute | solution.py:71
  289.9 14.3 %collective-permute-done.3 = f32[64,1024]{1,0:T(8,128)S(1)} collective-permute-done((f32[64,1024]{1,0:T(8,128)S(1)}, f32[64,1024]{1,0:T(8,128)S(1)}, u32[]{:S(2)}, u32[]{:S(2)}) %collective-permute-start.3) | collective-permute-done | bytes 262176 | tf_op jit(solution)/shard_map/ppermute | solution.py:71
  305.6 12.0 %all_to_all.11 = f32[32,1,1]{2,1,0:T(1,128)S(1)} all-to-all(f32[32,1,1]{2,1,0:T(1,128)S(1)} %broadcast_in_dim.5), channel_id=1, replica_groups=mesh['grp'=16,'cand'=32] {'cand'}, dimensions={0} | all-to-all | bytes 256 | tf_op jit(solution)/shard_map/all_to_all | solution.py:25
  (39 shorter events, 6.8 us)
Async XLA Ops:
  7.2 71.0 %copy-start = (bf16[24,32,1024]{2,1,0:T(8,128)(2,1)S(1)}, bf16[24,32,1024]{2,1,0:T(8,128)(2,1)}, u32[]{:S(2)}) copy-start(bf16[24,32,1024]{2,1,0:T(8,128)(2,1)} %param.6) | copy-start | bytes 4718596
  7.2 71.0 %all-gather.2.cloned.1.call-start = ((), (), s32[]{:S(2)}) async-start(), calls=%async_computation.3 | async-start | bytes 4325376 | tf_op jit(solution)/shard_map/all_gather | solution.py:81
  83.5 2.6 copy-start.6
  86.1 8.6 %copy-start.1 = (s32[24,32]{1,0:T(8,128)S(1)}, s32[24,32]{1,0:T(8,128)}, u32[]{:S(2)}) copy-start(s32[24,32]{1,0:T(8,128)} %param.10) | copy-start | bytes 9220
  86.1 8.6 %copy-start.2 = (s32[24,32]{1,0:T(8,128)S(1)}, s32[24,32]{1,0:T(8,128)}, u32[]{:S(2)}) copy-start(s32[24,32]{1,0:T(8,128)} %param.9) | copy-start | bytes 9220
  86.1 8.6 %copy-start.3 = (bf16[2048]{0:T(1024)(128)(2,1)S(1)}, bf16[2048]{0:T(1024)(128)(2,1)}, u32[]{:S(2)}) copy-start(bf16[2048]{0:T(1024)(128)(2,1)} %param.8) | copy-start | bytes 12292
  86.1 17.7 %copy-start.5 = (f32[24]{0:T(128)S(1)}, f32[24]{0:T(128)}, u32[]{:S(2)}) copy-start(f32[24]{0:T(128)} %param.11) | copy-start | bytes 292
  89.3 12.7 %all-to-all-start = ((f32[32,1,768]{2,1,0:T(1,128)}), f32[32,1,768]{2,1,0:T(1,128)S(1)}, u32[]{:S(2)}, u32[]{:S(2)}) async-start(f32[32,1,768]{2,1,0:T(1,128)} %reshape.24), calls=%async_computation | async-start | bytes 196608 | tf_op jit(solution)/shard_map/all_to_all | solution.py:25
  94.6 124.2 %reduce-scatter.2.cloned.1.call-start = ((), (), s32[]{:S(2)}) async-start(), calls=%async_computation.4 | async-start | bytes 4325376 | tf_op jit(solution)/shard_map/reduce_scatter | solution.py:104
  106.8 10.5 %copy-start.4 = (f32[24,32]{1,0:T(8,128)}, f32[24,32]{1,0:T(8,128)S(1)}, u32[]{:S(2)}) copy-start(f32[24,32]{1,0:T(8,128)S(1)} %fusion.13) | copy-start | bytes 9220
  219.7 7.1 %collective-permute-start = (f32[64,1024]{1,0:T(8,128)S(1)}, f32[64,1024]{1,0:T(8,128)S(1)}, u32[]{:S(2)}, u32[]{:S(2)}) collective-permute-start(f32[64,1024]{1,0:T(8,128)S(1)} %convert_element_type.37), channel_id=1, source_target_pairs={{0,32},{32,0},{64,96},{96,64},{128,160},{160,128},{192,224},{224,1... | collective-permute-start | bytes 786440 | tf_op jit(solution)/shard_map/ppermute | solution.py:71
  227.8 15.6 %collective-permute-start.1 = (f32[64,1024]{1,0:T(8,128)S(1)}, f32[64,1024]{1,0:T(8,128)S(1)}, u32[]{:S(2)}, u32[]{:S(2)}) collective-permute-start(f32[64,1024]{1,0:T(8,128)S(1)} %convert_add_fusion), channel_id=1, source_target_pairs={{0,64},{32,96},{64,0},{96,32},{128,192},{160,224},{192,128},{224,1... | collective-permute-start | bytes 786440 | tf_op jit(solution)/shard_map/ppermute | solution.py:71
  243.4 30.0 %collective-permute-start.2 = (f32[64,1024]{1,0:T(8,128)S(1)}, f32[64,1024]{1,0:T(8,128)S(1)}, u32[]{:S(2)}, u32[]{:S(2)}) collective-permute-start(f32[64,1024]{1,0:T(8,128)S(1)} %add.51), channel_id=1, source_target_pairs={{0,128},{32,160},{64,192},{96,224},{128,0},{160,32},{192,64},{224,... | collective-permute-start | bytes 786440 | tf_op jit(solution)/shard_map/ppermute | solution.py:71
  273.4 30.9 %collective-permute-start.3 = (f32[64,1024]{1,0:T(8,128)S(1)}, f32[64,1024]{1,0:T(8,128)S(1)}, u32[]{:S(2)}, u32[]{:S(2)}) collective-permute-start(f32[64,1024]{1,0:T(8,128)S(1)} %add.52), channel_id=1, source_target_pairs={{0,256},{32,288},{64,320},{96,352},{128,384},{160,416},{192,448},{... | collective-permute-start | bytes 786440 | tf_op jit(solution)/shard_map/ppermute | solution.py:71
Sparse Core Ops, SparseCore 0:
  11.1 67.0 all-gather.1
  117.4 101.2 reduce-scatter.1
